TPU v7x, 256 devices: a 2x2x32 block of a 4x8x32 slice. The times are simulated.
256 devices in a mesh: gp: 4 (over y, x), blk: 64 (over z, core).
Axes of the slice: x: 2, y: 2, z: 32, core: 2. Of those that a mesh axis runs over, the one named last changes fastest.
The devices are a block of a 4x8x32 slice.
Arguments:
- points: float32 [8, 65536], P(None, ('gp', 'blk')), parts along dimension 1, may hold values from -6 to 6
- vectors: float32 [8, 65536], P(None, ('gp', 'blk')), parts along dimension 1, may hold values from -6 to 6
- inv_length: float32 [32], P('gp'), parts along dimension 0, may hold values from 0.15 to 0.6
- noise: float32 [4], P('gp'), parts along dimension 0, may hold values from 0.1 to 1
Outputs:
- product: float32 [8, 65536], P(None, ('gp', 'blk')), parts along dimension 1
There are 4 independent parts, one for each index of `gp`. A program takes and returns all parts, laid end to end along the dimension named above; each array names one. Nothing has to cross between parts.
All inputs are finite; a program needn't handle non-finite values.
Results may differ from a plain program's by a relative error of at most 0.00017.
Values sent between devices are 32-bit elements; how exact they have to be, the bound alone decides.
A program may use at most 64 MiB of HBM per device.

v0:
```python
import jax
import jax.numpy as jnp
from jax import lax
from jax.sharding import PartitionSpec as P


def matern(left, right, inv_length):
    scaled_left = left * inv_length[:, None]
    scaled_right = right * inv_length[:, None]
    sq_left = jnp.sum(scaled_left * scaled_left, axis=0)
    sq_right = jnp.sum(scaled_right * scaled_right, axis=0)
    cross = jnp.dot(
        scaled_left.T,
        scaled_right,
        precision=lax.Precision.HIGHEST,
        preferred_element_type=jnp.float32,
    )
    dist2 = jnp.maximum(sq_left[:, None] + sq_right[None, :] - 2.0 * cross, 0.0)
    scaled_dist = jnp.sqrt(5.0 * dist2)
    return (1.0 + scaled_dist + scaled_dist * scaled_dist / 3.0) * jnp.exp(-scaled_dist)


def apply_tile(vec_other, tile):
    return jnp.dot(
        vec_other, tile, precision=lax.Precision.HIGHEST, preferred_element_type=jnp.float32
    )


def on_device(points, vectors, inv_length, noise):
    count = lax.axis_size("blk")
    total_points = points.shape[1] * count
    tile = matern(lax.all_gather(points, "blk", axis=1, tiled=True), points, inv_length)
    own_sum = apply_tile(lax.all_gather(vectors, "blk", axis=1, tiled=True), tile)
    return noise[0] * vectors + own_sum / jnp.sqrt(jnp.float32(total_points))


def solution(mesh):
    return jax.shard_map(
        on_device,
        mesh=mesh,
        in_specs=(P(None, ("gp", "blk")), P(None, ("gp", "blk")), P("gp"), P("gp")),
        out_specs=P(None, ("gp", "blk")),
        check_vma=False,
    )
```

profile of v0, /device:TPU:37, one launch (start us, length us, event | category | flops | bytes accessed | tf_op | source)
XLA Modules:
  0.0 170.3 jit_solution(1310754627161676833)
XLA Ops:
  0.0 0.0 copy-start
  0.0 78.1 %all_gather.6 = f32[8,16384]{1,0:T(8,128)S(1)} all-gather(f32[8,256]{1,0:T(8,128)} %param.4), channel_id=1, replica_groups=mesh['gp'=4,'blk'=64] {'blk'}, dimensions={1}, use_global_device_ids=true | all-gather | bytes 532480 | tf_op jit(solution)/shard_map/all_gather | solution.py:32
  78.1 0.9 multiply_reduce_fusion
  79.0 0.8 multiply_reduce_fusion.1
  79.8 23.7 %fusion.3 = f32[16384,256]{1,0:T(8,128)S(1)} fusion(f32[256]{0:T(256)S(1)} %multiply_reduce_fusion.1, f32[16384]{0:T(1024)S(1)} %multiply_reduce_fusion, f32[8,16384]{1,0:T(8,128)S(1)} %all_gather.6, f32[8]{0:T(128)} %param.6, f32[8,256]{1,0:T(8,128)} %param.4), kind=kOutput, calls=%fused_computation.4 | convolution fusion | flops 423757824 | bytes 17376288 | tf_op jit(solution)/shard_map/dot_general | solution.py:12
  103.5 0.0 copy-done
  103.5 54.1 %all_gather.7 = f32[8,16384]{1,0:T(8,128)S(1)} all-gather(f32[8,256]{1,0:T(8,128)S(1)} %copy-done), channel_id=1, replica_groups=mesh['gp'=4,'blk'=64] {'blk'}, dimensions={1}, use_global_device_ids=true | all-gather | bytes 532480 | tf_op jit(solution)/shard_map/all_gather | solution.py:33
  158.2 12.1 %fusion.20 = f32[8,256]{1,0:T(8,128)} fusion(f32[8,16384]{1,0:T(8,128)S(1)} %all_gather.7, f32[16384,256]{1,0:T(8,128)S(1)} %fusion.3, f32[8,256]{1,0:T(8,128)S(1)} %copy-done, f32[]{:T(128)} %bitcast.6), kind=kOutput, calls=%fused_computation.17 | convolution fusion | flops 427825152 | bytes 17317892 | tf_op jit(solution)/shard_map/dot_general | solution.py:24
Async XLA Ops:
  0.0 103.5 %copy-start = (f32[8,256]{1,0:T(8,128)S(1)}, f32[8,256]{1,0:T(8,128)}, u32[]{:S(2)}) copy-start(f32[8,256]{1,0:T(8,128)} %param.5) | copy-start | bytes 24580
where the time goes:
time: 171 us; the launch traced here: 170 us
  blocking collectives  132 us (77%)
  matrix products  35.8 us (21%)
    all_gather x1, blocking collectives, on_device(): lax.all_gather(points, 'blk', axis=1, tiled=True)  78.1 us
    all_gather x1, blocking collectives, on_device(): lax.all_gather(vectors, 'blk', axis=1, tiled=True)  54.1 us
    dot_general x1, matrix products, matern(): jnp.dot(scaled_left.T, scaled_right, precision=lax.Precision.HIGHEST, pre...  23.7 us
    dot_general x1, matrix products, apply_tile(): jnp.dot(vec_other, tile, precision=lax.Precision.HIGHEST, preferred_eleme...  12.1 us

commit v1 on v0

v1 whole, which is shorter than its diff:
```python
import functools
import math

import jax
import jax.numpy as jnp
from jax import lax
from jax.experimental import pallas as pl
from jax.experimental.pallas import tpu as pltpu
from jax.sharding import PartitionSpec as P

NEAR = 8
ROWS = 128
LN2 = math.log(2.0)
UNIT = LN2 * LN2 / 3.0
TINY = 1e-30
MESH = pl.DeviceIdType.MESH
F32, BF16 = jnp.float32, jnp.bfloat16


def split(x, count):
    parts = []
    for _ in range(count):
        part = x.astype(BF16).astype(F32)
        parts.append(part)
        x = x - part
    return parts


def factors(scaled):
    sq = jnp.sum(scaled * scaled, axis=0, keepdims=True)
    hi, mid, low = split(scaled, 3)
    sq_parts = split(sq, 3)
    row = lax.broadcasted_iota(jnp.int32, scaled.shape, 0)
    first = jnp.where(row == 0, sq_parts[0], jnp.where(row == 1, sq_parts[1], jnp.where(row == 2, sq_parts[2], 0.0)))
    left_sq = jnp.where((row >= 3) & (row < 6), 1.0, first)
    second = jnp.where(row == 3, sq_parts[0], jnp.where(row == 4, sq_parts[1], jnp.where(row == 5, sq_parts[2], 0.0)))
    right_sq = jnp.where(row < 3, 1.0, second)
    return [hi, hi, mid, hi, low, mid, left_sq], [-2.0 * hi, -2.0 * mid, -2.0 * hi, -2.0 * low, -2.0 * hi, -2.0 * mid, right_sq]


def put_rows(points, inv, left_ref, start):
    left, _ = factors(points * inv)
    left = jnp.concatenate(left + [jnp.zeros_like(points)], axis=0)
    left_ref[pl.ds(start, points.shape[1]), :] = left.T.astype(BF16)


def add_block(block_ref, inv, left_ref, acc_ref):
    dim = block_ref.shape[0] // 2
    points, vectors = block_ref[:dim, :], block_ref[dim:, :]
    _, right = factors(points * inv)
    right = jnp.concatenate(right + [jnp.zeros_like(points)], axis=0).astype(BF16)
    vec_parts = jnp.concatenate(split(vectors, 2), axis=0).astype(BF16)
    vec_parts = jnp.concatenate([vec_parts, vec_parts], axis=1)
    for start in range(0, left_ref.shape[0], ROWS):
        rows = pl.ds(start, ROWS)
        squared = jnp.maximum(jnp.dot(left_ref[rows, :], right, preferred_element_type=F32), TINY)
        dist = squared * lax.rsqrt(squared)
        kern = (dist * (dist + 3.0 / LN2) + 3.0 / (LN2 * LN2)) * jnp.exp2(-dist)
        high = kern.astype(BF16)
        low = (kern - high.astype(F32)).astype(BF16)
        both = jnp.concatenate([high, low], axis=1)
        added = lax.dot_general(both, vec_parts, (((1,), (1,)), ((), ())), preferred_element_type=F32)
        acc_ref[rows, :] = acc_ref[rows, :] + added


def kernel(
    count, inv_ref, points_ref, vectors_ref, out_ref,
    blocks, near, left_ref, acc_ref, sums, sums_in,
    own_sem, far_send, far_recv, near_send, near_recv, sum_send, sum_recv,
):
    me = lax.axis_index("blk")
    member = lax.rem(me, NEAR)
    base = me - member
    dim, points = points_ref.shape
    above, below = lax.rem(me + NEAR, count), lax.rem(me + count - NEAR, count)
    ups = count // NEAR // 2
    downs = count // NEAR - 1 - ups

    own = [
        pltpu.make_async_copy(points_ref, blocks.at[0, pl.ds(0, dim)], own_sem.at[0]),
        pltpu.make_async_copy(vectors_ref, blocks.at[0, pl.ds(dim, dim)], own_sem.at[1]),
        pltpu.make_async_copy(points_ref, near.at[member], own_sem.at[2]),
    ]
    for copy in own:
        copy.start()

    def other(k):
        return base + lax.rem(member + k, NEAR)

    barrier = pltpu.get_barrier_semaphore()
    for peer in [above, below] + [other(k) for k in range(1, NEAR)]:
        pl.semaphore_signal(barrier, inc=1, device_id={"blk": peer}, device_id_type=MESH)

    def remote(source, target, sends, recvs, i_send, i_recv, peer):
        return pltpu.make_async_remote_copy(
            src_ref=source, dst_ref=target, send_sem=sends.at[i_send], recv_sem=recvs.at[i_recv],
            device_id={"blk": peer}, device_id_type=MESH,
        )

    def up(k):
        return remote(blocks.at[k - 1], blocks.at[k], far_send, far_recv, k, k, above)

    def down(k):
        source = 0 if k == 1 else ups + k - 1
        return remote(blocks.at[source], blocks.at[ups + k], far_send, far_recv, ups + k, ups + k, below)

    def points_to(k):
        return remote(blocks.at[0, pl.ds(0, dim)], near.at[member], near_send, near_recv, k, member, other(k))

    def points_from(k):
        return remote(blocks.at[0, pl.ds(0, dim)], near.at[other(k) - base], near_send, near_recv, k, other(k) - base, other(k))

    def sums_to(k):
        return remote(sums.at[other(k) - base], sums_in.at[member], sum_send, sum_recv, k, member, other(k))

    def sums_from(k):
        return remote(sums.at[0], sums_in.at[other(k) - base], sum_send, sum_recv, k, other(k) - base, other(k))

    row = lax.broadcasted_iota(jnp.int32, (dim, points), 0)
    inv = jnp.zeros((dim, points), F32)
    for d in range(dim):
        inv = jnp.where(row == d, inv_ref[d] * (math.sqrt(5.0) / LN2), inv)
    acc_ref[...] = jnp.zeros_like(acc_ref)

    for copy in own:
        copy.wait()
    pl.semaphore_wait(barrier, NEAR + 1)
    up(1).start()
    down(1).start()
    for k in range(1, NEAR):
        points_to(k).start()
    for k in range(1, NEAR):
        points_from(k).wait_recv()

    @pl.loop(0, NEAR)
    def _(m):
        put_rows(near[m], inv, left_ref, pl.multiple_of(m * points, points))

    @pl.loop(0, count // NEAR)
    def _(step):
        for k in range(1, ups + 1):
            @pl.when(step == (2 * k - 3 if k > 1 else 0) if k < ups or downs == ups else step == 2 * k - 1)
            def _():
                up(k).wait_recv()
                if k < ups:
                    up(k + 1).start()
                if k <= downs:
                    down(k).wait_recv()
                    if k < downs:
                        down(k + 1).start()

        stage = (step + 1) // 2
        slot = jnp.where((step > 0) & (lax.rem(step, 2) == 0), ups + stage, stage)
        add_block(blocks.at[slot], inv, left_ref, acc_ref)

    @pl.loop(0, NEAR)
    def _(m):
        both = acc_ref[pl.ds(pl.multiple_of(m * points, points), points), :].T
        sums[m] = both[:dim] + both[dim:]

    for k in range(1, NEAR):
        sums_to(k).start()
    sums_in[member] = sums[member]
    for k in range(1, NEAR):
        sums_from(k).wait_recv()
    total = sums_in[0]
    for m in range(1, NEAR):
        total = total + sums_in[m]
    out_ref[...] = total

    for k in range(1, ups + 1):
        up(k).wait_send()
    for k in range(1, downs + 1):
        down(k).wait_send()
    for k in range(1, NEAR):
        points_to(k).wait_send()
        sums_to(k).wait_send()


def on_device(points, vectors, inv_length, noise):
    count = lax.axis_size("blk")
    dim, size = points.shape
    rhs = vectors.shape[0]
    groups = count // NEAR
    total = pl.pallas_call(
        functools.partial(kernel, count),
        out_shape=jax.ShapeDtypeStruct(vectors.shape, F32),
        in_specs=[
            pl.BlockSpec(memory_space=pltpu.SMEM),
            pl.BlockSpec(memory_space=pl.ANY),
            pl.BlockSpec(memory_space=pl.ANY),
        ],
        out_specs=pl.BlockSpec(memory_space=pltpu.VMEM),
        scratch_shapes=[
            pltpu.VMEM((groups, dim + rhs, size), F32),
            pltpu.VMEM((NEAR, dim, size), F32),
            pltpu.VMEM((NEAR * size, 8 * dim), BF16),
            pltpu.VMEM((NEAR * size, 2 * rhs), F32),
            pltpu.VMEM((NEAR, rhs, size), F32),
            pltpu.VMEM((NEAR, rhs, size), F32),
            pltpu.SemaphoreType.DMA((3,)),
            pltpu.SemaphoreType.DMA((groups,)),
            pltpu.SemaphoreType.DMA((groups,)),
            pltpu.SemaphoreType.DMA((NEAR,)),
            pltpu.SemaphoreType.DMA((NEAR,)),
            pltpu.SemaphoreType.DMA((NEAR,)),
            pltpu.SemaphoreType.DMA((NEAR,)),
        ],
        compiler_params=pltpu.CompilerParams(collective_id=0, has_side_effects=True),
        name="matern_product",
    )(inv_length, points, vectors)
    return noise[0] * vectors + total * (UNIT / math.sqrt(size * count))


def solution(mesh):
    return jax.shard_map(
        on_device,
        mesh=mesh,
        in_specs=(P(None, ("gp", "blk")), P(None, ("gp", "blk")), P("gp"), P("gp")),
        out_specs=P(None, ("gp", "blk")),
        check_vma=False,
    )
```

time: 171 us -> 64.8 us (0.38)
  blocking collectives: 132 us -> 0 us
  Pallas kernels: 0 us -> 62.5 us
  matrix products: 35.8 us -> 0 us
    all_gather x2 -> x0, blocking collectives: 132 us -> none  [the longest x1 78.1 us: on_device(): lax.all_gather(points, 'blk', axis=1, tiled=True)]
    pallas_call x0 -> x1, Pallas kernels: none -> 62.5 us  [on_device(): pl.pallas_call(functools.partial(kernel, count), out_shape=jax.ShapeDtype...]
    dot_general x2 -> x0, matrix products: 35.8 us -> none  [the longest x1 23.7 us: matern(): jnp.dot(scaled_left.T, scaled_right, precision=lax.Precision.HIGHEST, pre...]
where the time goes in v1:
time: 64.8 us; the launch traced here: 64.5 us
  Pallas kernels  62.5 us (96%)
  other arithmetic  1.3 us (2%)
  between operations  0.68 us (1%)
    pallas_call x1, Pallas kernels, on_device(): pl.pallas_call(functools.partial(kernel, count), out_shape=jax.ShapeDtype...  62.5 us
    add x1, other arithmetic, on_device(): return noise[0] * vectors + total * (UNIT / math.sqrt(size * count))  1.3 us

profile of v1, /device:TPU:37, one launch (start us, length us, event | category | flops | bytes accessed | tf_op | source)
XLA Modules:
  0.0 64.5 jit_solution(6682945153657272750)
XLA Ops:
  0.7 0.0 copy-start
  0.7 62.5 %matern_product.1 = f32[8,256]{1,0:T(8,128)} custom-call(f32[8]{0:T(128)} %inv_ref.1, f32[8,256]{1,0:T(8,128)} %points_ref.1, f32[8,256]{1,0:T(8,128)} %vectors_ref.1), custom_call_target="tpu_custom_call" | custom-call | tf_op jit(solution)/shard_map/matern_product/pallas_call | solution.py:185
  63.2 0.0 copy-done
  63.2 1.3 %multiply_add_fusion = f32[8,256]{1,0:T(8,128)} fusion(f32[8,256]{1,0:T(8,128)} %matern_product.1, f32[8,256]{1,0:T(8,128)S(1)} %copy-done, f32[]{:T(128)} %bitcast.1), kind=kLoop, calls=%fused_computation | loop fusion | flops 6144 | bytes 24580 | tf_op jit(solution)/shard_map/add | solution.py:212
Async XLA Ops:
  0.7 62.6 %copy-start = (f32[8,256]{1,0:T(8,128)S(1)}, f32[8,256]{1,0:T(8,128)}, u32[]{:S(2)}) copy-start(f32[8,256]{1,0:T(8,128)} %vectors_ref.1) | copy-start | bytes 24580

commit v2 on v1

--- a/solution.py
+++ b/solution.py
@@ -9,9 +9,9 @@
 from jax.sharding import PartitionSpec as P
 
 NEAR = 8
-ROWS = 128
+COLS = 256
 LN2 = math.log(2.0)
-UNIT = LN2 * LN2 / 3.0
+UNIT = 3.0
 TINY = 1e-30
 MESH = pl.DeviceIdType.MESH
 F32, BF16 = jnp.float32, jnp.bfloat16
@@ -38,34 +38,35 @@
     return [hi, hi, mid, hi, low, mid, left_sq], [-2.0 * hi, -2.0 * mid, -2.0 * hi, -2.0 * low, -2.0 * hi, -2.0 * mid, right_sq]
 
 
-def put_rows(points, inv, left_ref, start):
-    left, _ = factors(points * inv)
-    left = jnp.concatenate(left + [jnp.zeros_like(points)], axis=0)
-    left_ref[pl.ds(start, points.shape[1]), :] = left.T.astype(BF16)
-
-
-def add_block(block_ref, inv, left_ref, acc_ref):
-    dim = block_ref.shape[0] // 2
-    points, vectors = block_ref[:dim, :], block_ref[dim:, :]
+def put_columns(points, inv, right_ref, start):
     _, right = factors(points * inv)
-    right = jnp.concatenate(right + [jnp.zeros_like(points)], axis=0).astype(BF16)
-    vec_parts = jnp.concatenate(split(vectors, 2), axis=0).astype(BF16)
-    vec_parts = jnp.concatenate([vec_parts, vec_parts], axis=1)
-    for start in range(0, left_ref.shape[0], ROWS):
-        rows = pl.ds(start, ROWS)
-        squared = jnp.maximum(jnp.dot(left_ref[rows, :], right, preferred_element_type=F32), TINY)
-        dist = squared * lax.rsqrt(squared)
-        kern = (dist * (dist + 3.0 / LN2) + 3.0 / (LN2 * LN2)) * jnp.exp2(-dist)
-        high = kern.astype(BF16)
-        low = (kern - high.astype(F32)).astype(BF16)
-        both = jnp.concatenate([high, low], axis=1)
-        added = lax.dot_general(both, vec_parts, (((1,), (1,)), ((), ())), preferred_element_type=F32)
-        acc_ref[rows, :] = acc_ref[rows, :] + added
+    right_ref[:, pl.ds(start, points.shape[1])] = jnp.concatenate(right + [jnp.zeros_like(points)], axis=0).astype(BF16)
+
+
+def add_blocks(block_refs, inv, right_ref, acc_ref):
+    lefts, vecs = [], []
+    for block_ref in block_refs:
+        dim = block_ref.shape[0] // 2
+        left, _ = factors(block_ref[:dim, :] * inv)
+        lefts.append(jnp.concatenate(left + [jnp.zeros_like(inv)], axis=0).T.astype(BF16))
+        vecs.append(jnp.concatenate(split(block_ref[dim:, :], 2), axis=0).astype(BF16))
+    for start in range(0, right_ref.shape[1], COLS):
+        cols = pl.ds(start, COLS)
+        added = acc_ref[:, cols]
+        for left, vec in zip(lefts, vecs):
+            squared = jnp.maximum(jnp.dot(left, right_ref[:, cols], preferred_element_type=F32), TINY)
+            dist = squared * lax.rsqrt(squared)
+            kern = (squared + dist + 1.0 / 3.0) * jnp.exp2(dist * (-3.0 / LN2))
+            high = kern.astype(BF16)
+            low = (kern - high.astype(F32)).astype(BF16)
+            added = added + jnp.dot(vec, high, preferred_element_type=F32)
+            added = added + jnp.dot(vec, low, preferred_element_type=F32)
+        acc_ref[:, cols] = added
 
 
 def kernel(
     count, inv_ref, points_ref, vectors_ref, out_ref,
-    blocks, near, left_ref, acc_ref, sums, sums_in,
+    blocks, near, right_ref, acc_ref, sums, sums_in,
     own_sem, far_send, far_recv, near_send, near_recv, sum_send, sum_recv,
 ):
     me = lax.axis_index("blk")
@@ -119,7 +120,7 @@
     row = lax.broadcasted_iota(jnp.int32, (dim, points), 0)
     inv = jnp.zeros((dim, points), F32)
     for d in range(dim):
-        inv = jnp.where(row == d, inv_ref[d] * (math.sqrt(5.0) / LN2), inv)
+        inv = jnp.where(row == d, inv_ref[d] * (math.sqrt(5.0) / 3.0), inv)
     acc_ref[...] = jnp.zeros_like(acc_ref)
 
     for copy in own:
@@ -134,28 +135,35 @@
 
     @pl.loop(0, NEAR)
     def _(m):
-        put_rows(near[m], inv, left_ref, pl.multiple_of(m * points, points))
-
-    @pl.loop(0, count // NEAR)
-    def _(step):
-        for k in range(1, ups + 1):
-            @pl.when(step == (2 * k - 3 if k > 1 else 0) if k < ups or downs == ups else step == 2 * k - 1)
+        put_columns(near[m], inv, right_ref, pl.multiple_of(m * points, points))
+
+    def pass_on(k):
+        up(k).wait_recv()
+        if k < ups:
+            up(k + 1).start()
+        if k <= downs:
+            down(k).wait_recv()
+            if k < downs:
+                down(k + 1).start()
+
+    if downs > 0:
+        pass_on(1)
+    add_blocks([blocks.at[0]], inv, right_ref, acc_ref)
+
+    @pl.loop(1, downs + 1)
+    def _(stage):
+        for k in range(2, downs + 1):
+            @pl.when(stage == k - 1)
             def _():
-                up(k).wait_recv()
-                if k < ups:
-                    up(k + 1).start()
-                if k <= downs:
-                    down(k).wait_recv()
-                    if k < downs:
-                        down(k + 1).start()
-
-        stage = (step + 1) // 2
-        slot = jnp.where((step > 0) & (lax.rem(step, 2) == 0), ups + stage, stage)
-        add_block(blocks.at[slot], inv, left_ref, acc_ref)
-
-    @pl.loop(0, NEAR)
-    def _(m):
-        both = acc_ref[pl.ds(pl.multiple_of(m * points, points), points), :].T
+                pass_on(k)
+        add_blocks([blocks.at[stage], blocks.at[ups + stage]], inv, right_ref, acc_ref)
+
+    if ups > downs:
+        pass_on(ups)
+        add_blocks([blocks.at[ups]], inv, right_ref, acc_ref)
+
+    for m in range(NEAR):
+        both = acc_ref[:, pl.ds(m * points, points)]
         sums[m] = both[:dim] + both[dim:]
 
     for k in range(1, NEAR):
@@ -194,8 +202,8 @@
         scratch_shapes=[
             pltpu.VMEM((groups, dim + rhs, size), F32),
             pltpu.VMEM((NEAR, dim, size), F32),
-            pltpu.VMEM((NEAR * size, 8 * dim), BF16),
-            pltpu.VMEM((NEAR * size, 2 * rhs), F32),
+            pltpu.VMEM((8 * dim, NEAR * size), BF16),
+            pltpu.VMEM((2 * rhs, NEAR * size), F32),
             pltpu.VMEM((NEAR, rhs, size), F32),
             pltpu.VMEM((NEAR, rhs, size), F32),
             pltpu.SemaphoreType.DMA((3,)),

time: 64.8 us -> 53.3 us (0.82)
  Pallas kernels: 62.5 us -> 51 us
    pallas_call x1, Pallas kernels: 62.5 us -> 51 us  [on_device(): pl.pallas_call(functools.partial(kernel, count), out_shape=jax.ShapeDtype...]
where the time goes in v2:
time: 53.3 us; the launch traced here: 53 us
  Pallas kernels  51 us (96%)
  other arithmetic  1.3 us (2%)
  between operations  0.68 us (1%)
    pallas_call x1, Pallas kernels, on_device(): pl.pallas_call(functools.partial(kernel, count), out_shape=jax.ShapeDtype...  51 us
    add x1, other arithmetic, on_device(): return noise[0] * vectors + total * (UNIT / math.sqrt(size * count))  1.3 us

profile of v2, /device:TPU:37, one launch (start us, length us, event | category | flops | bytes accessed | tf_op | source)
XLA Modules:
  0.0 53.0 jit_solution(17994650458202720082)
XLA Ops:
  0.7 0.0 copy-start
  0.7 51.0 %matern_product.1 = f32[8,256]{1,0:T(8,128)} custom-call(f32[8]{0:T(128)} %inv_ref.1, f32[8,256]{1,0:T(8,128)} %points_ref.1, f32[8,256]{1,0:T(8,128)} %vectors_ref.1), custom_call_target="tpu_custom_call" | custom-call | tf_op jit(solution)/shard_map/matern_product/pallas_call | solution.py:193
  51.7 0.0 copy-done
  51.7 1.3 %multiply_add_fusion = f32[8,256]{1,0:T(8,128)} fusion(f32[8,256]{1,0:T(8,128)} %matern_product.1, f32[8,256]{1,0:T(8,128)S(1)} %copy-done, f32[]{:T(128)} %bitcast.1), kind=kLoop, calls=%fused_computation | loop fusion | flops 6144 | bytes 24580 | tf_op jit(solution)/shard_map/add | solution.py:220
Async XLA Ops:
  0.7 51.0 %copy-start = (f32[8,256]{1,0:T(8,128)S(1)}, f32[8,256]{1,0:T(8,128)}, u32[]{:S(2)}) copy-start(f32[8,256]{1,0:T(8,128)} %vectors_ref.1) | copy-start | bytes 24580
